TPU v7x, 512 devices: a whole 4x4x16 slice. The times are simulated.
512 devices in a mesh: box: 16 (over z), row: 4 (over y_hi, core), col: 8 (over x, y_lo).
Axes of the slice: x: 4, y: 4 (y_hi: 2, y_lo: 2; y = y_hi * 2 + y_lo), z: 16, core: 2. Of those that a mesh axis runs over, the one named last changes fastest.
Arguments:
- ext_ext: float32 [16, 3072, 3072], P('box', 'row', 'col'), may hold values from -6 to 6
- ext_int: float32 [16, 3072, 1024], P('box', 'row', 'col'), may hold values from -0.1875 to 0.1875
- int_ext: float32 [16, 1024, 3072], P('box', 'row', 'col'), may hold values from -6 to 6
- int_int: float32 [16, 1024, 1024], P('box', 'row', 'col'), may hold values from -0.1 to 0.1, as said below
Outputs:
- merged: float32 [16, 3072, 2, 3072], P('box', 'row', None, 'col')
Inputs may be any that keep to these rules, and one draw needn't show every extreme that they name: `int_int`: independent entries.
All inputs are finite; a program needn't handle non-finite values.
Results may differ from a plain program's by a relative error of at most 0.0003.
Values sent between devices are 32-bit elements; how exact they have to be, the bound alone decides.
A program may use at most 64 MiB of HBM per device.

v0:
```python
import jax
import jax.numpy as jnp
from jax import lax
from jax.sharding import PartitionSpec as P

HIGH = lax.Precision.HIGHEST


def in_order(pieces, dim):
    pieces = jnp.moveaxis(pieces, 0, dim)
    dims = pieces.shape
    return pieces.reshape(*dims[:dim], dims[dim] * dims[dim + 1], *dims[dim + 2 :])


def sent_to_all(shard, axis):
    devices = lax.axis_size(axis)
    return lax.all_to_all(
        jnp.broadcast_to(shard[None], (devices, *shard.shape)), axis, 0, 0, tiled=True
    )


def gathered_copies(shard, axis, dim):
    return in_order(sent_to_all(shard, axis), dim)


def swapped(shard, axis, distance):
    return lax.ppermute(shard, axis, [(i, i ^ 1 << distance) for i in range(lax.axis_size(axis))])


def panel_dot(total, piece, panel):
    return total + jnp.dot(piece, panel, precision=HIGH, preferred_element_type=jnp.float32)


def chain_product(left, right):
    panel = gathered_copies(right, "row", 0)
    empty = jnp.zeros((left.shape[0], right.shape[1]), jnp.float32)
    return panel_dot(empty, gathered_copies(left, "col", 1), panel)


def local(ext_ext, ext_int, int_ext, int_int):
    own_ee = ext_ext[0]
    own_ed = ext_int[0]
    own_de = int_ext[0]
    own_dd = int_int[0]
    partner_dd, partner_de = swapped((own_dd, own_de), "box", 0)
    is_even = lax.axis_index("box") % 2 == 0
    block_rows = own_dd.shape[0]
    block_cols = own_dd.shape[1]
    row_ids = lax.axis_index("row") * block_rows + lax.broadcasted_iota(
        jnp.int32, (block_rows, block_cols), 0
    )
    col_ids = lax.axis_index("col") * block_cols + lax.broadcasted_iota(
        jnp.int32, (block_rows, block_cols), 1
    )
    identity = (row_ids == col_ids).astype(jnp.float32)
    coupling = chain_product(partner_dd, own_dd)
    square = chain_product(coupling, coupling)
    first = identity + coupling
    inverse = first + chain_product(first, square)
    de_panel = gathered_copies(own_de, "row", 0)
    coupled = panel_dot(
        jnp.zeros(own_de.shape, jnp.float32), gathered_copies(partner_dd, "col", 1), de_panel
    )
    source = jnp.concatenate(
        [jnp.where(is_even, coupled, partner_de), jnp.where(is_even, partner_de, coupled)], axis=1
    )
    source_panel = lax.all_gather(source, "row", axis=0, tiled=True)
    carried = panel_dot(
        jnp.zeros(source.shape, jnp.float32), gathered_copies(inverse, "col", 1), source_panel
    )
    right_panel = lax.all_gather(carried, "row", axis=0, tiled=True)
    zeros = jnp.zeros_like(own_ee)
    start_terms = jnp.concatenate(
        [jnp.where(is_even, own_ee, zeros), jnp.where(is_even, zeros, own_ee)], axis=1
    )
    merged = panel_dot(start_terms, lax.all_gather(own_ed, "col", axis=1, tiled=True), right_panel)
    return merged.reshape(1, own_ee.shape[0], 2, own_ee.shape[1])


def solution(mesh):
    placed = (
        P("box", "row", "col"),
        P("box", "row", "col"),
        P("box", "row", "col"),
        P("box", "row", "col"),
    )
    return jax.shard_map(
        local, mesh=mesh, in_specs=placed, out_specs=P("box", "row", None, "col"), check_vma=False
    )
```

profile of v0, /device:TPU:1, one launch (start us, length us, event | category | flops | bytes accessed | tf_op | source)
XLA Modules:
  0.0 298.8 jit_solution(4053123968927167016)
XLA Ops:
  6.5 0.0 copy-start.1
  6.5 4.5 %collective-permute-start = (f32[256,128]{1,0:T(8,128)}, f32[256,128]{1,0:T(8,128)S(1)}, u32[]{:S(2)}, u32[]{:S(2)}) collective-permute-start(f32[256,128]{1,0:T(8,128)} %bitcast.53), channel_id=1, source_target_pairs={{0,32},{32,0},{64,96},{96,64},{128,160},{160,128},{192,224},{224,1... | collective-permute-start | bytes 393224 | tf_op jit(solution)/shard_map/ppermute | solution.py:27
  11.0 2.6 collective-permute-done
  13.6 0.1 copy.10
  13.7 0.1 broadcast_in_dim.21
  13.8 17.0 %all_to_all.41 = f32[8,256,128]{1,2,0:T(8,128)S(1)} all-to-all(f32[8,256,128]{1,2,0:T(8,128)S(1)} %broadcast_in_dim.21), channel_id=1, replica_groups=mesh['box'=16,'row'=4,'col'=8] {'col'}, dimensions={0} | all-to-all | bytes 2097152 | tf_op jit(solution)/shard_map/all_to_all | solution.py:17
  30.8 0.0 copy-done.1
  30.8 1.2 broadcast_in_dim.29
  32.0 9.1 %all-to-all-start.7 = ((f32[4,256,384]{2,1,0:T(8,128)}), f32[4,256,384]{2,1,0:T(8,128)S(1)}, u32[]{:S(2)}, u32[]{:S(2)}) async-start(f32[4,256,384]{2,1,0:T(8,128)} %broadcast_in_dim.29), calls=%async_computation.7 | async-start | bytes 3145728 | tf_op jit(solution)/shard_map/all_to_all | solution.py:17
  41.1 0.0 all-gather.5.cloned.1.call-start
  41.1 3.2 %collective-permute-start.1 = (f32[256,384]{1,0:T(8,128)S(1)}, f32[256,384]{1,0:T(8,128)S(1)}, u32[]{:S(2)}, u32[]{:S(2)}) collective-permute-start(f32[256,384]{1,0:T(8,128)S(1)} %bitcast.52), channel_id=1, source_target_pairs={{0,32},{32,0},{64,96},{96,64},{128,160},{160,128},{192,224},{224,1... | collective-permute-start | bytes 1179656 | tf_op jit(solution)/shard_map/ppermute | solution.py:27
  44.3 9.4 %collective-permute-done.1 = f32[256,384]{1,0:T(8,128)S(1)} collective-permute-done((f32[256,384]{1,0:T(8,128)S(1)}, f32[256,384]{1,0:T(8,128)S(1)}, u32[]{:S(2)}, u32[]{:S(2)}) %collective-permute-start.1) | collective-permute-done | bytes 393248 | tf_op jit(solution)/shard_map/ppermute | solution.py:27
  53.6 8.0 %all-to-all-done.7 = f32[4,256,384]{2,1,0:T(8,128)S(1)} async-done(((f32[4,256,384]{2,1,0:T(8,128)}), f32[4,256,384]{2,1,0:T(8,128)S(1)}, u32[]{:S(2)}, u32[]{:S(2)}) %all-to-all-start.7) | async-done | bytes 1572896 | tf_op jit(solution)/shard_map/all_to_all | solution.py:17
  61.7 0.0 copy-start.2
  61.7 1.9 broadcast_select_fusion.1
  63.5 0.9 pad_maximum_fusion
  64.5 0.0 all-gather.5.cloned.1.call-update
  64.5 0.0 all-gather.9.cloned.1.call-start
  64.5 0.7 all-gather.9.cloned.1.call-update
  65.3 0.0 copy-done.2
  65.3 0.8 broadcast_in_dim.22
  66.1 4.4 %all-to-all-start.1 = ((f32[4,256,128]{2,1,0:T(8,128)}), f32[4,256,128]{2,1,0:T(8,128)S(1)}, u32[]{:S(2)}, u32[]{:S(2)}) async-start(f32[4,256,128]{2,1,0:T(8,128)} %broadcast_in_dim.22), calls=%async_computation.1 | async-start | bytes 1048576 | tf_op jit(solution)/shard_map/all_to_all | solution.py:17
  70.5 9.3 %all-to-all-done.1 = f32[4,256,128]{2,1,0:T(8,128)S(1)} async-done(((f32[4,256,128]{2,1,0:T(8,128)}), f32[4,256,128]{2,1,0:T(8,128)S(1)}, u32[]{:S(2)}, u32[]{:S(2)}) %all-to-all-start.1) | async-done | bytes 524320 | tf_op jit(solution)/shard_map/all_to_all | solution.py:17
  79.9 1.8 convert_add_fusion
  81.7 0.8 broadcast_in_dim.25
  82.5 4.4 %all-to-all-start.4 = ((f32[4,256,128]{2,1,0:T(8,128)}), f32[4,256,128]{2,1,0:T(8,128)S(1)}, u32[]{:S(2)}, u32[]{:S(2)}) async-start(f32[4,256,128]{2,1,0:T(8,128)} %broadcast_in_dim.25), calls=%async_computation.4 | async-start | bytes 1048576 | tf_op jit(solution)/shard_map/all_to_all | solution.py:17
  86.9 0.1 copy.12
  87.0 15.5 %all-to-all-done.4 = f32[4,256,128]{2,1,0:T(8,128)S(1)} async-done(((f32[4,256,128]{2,1,0:T(8,128)}), f32[4,256,128]{2,1,0:T(8,128)S(1)}, u32[]{:S(2)}, u32[]{:S(2)}) %all-to-all-start.4) | async-done | bytes 524320 | tf_op jit(solution)/shard_map/all_to_all | solution.py:17
  102.5 1.1 broadcast_in_dim.24
  103.6 3.6 %all-to-all-start.3 = ((f32[8,256,128]{1,2,0:T(8,128)}), f32[8,256,128]{1,2,0:T(8,128)S(1)}, u32[]{:S(2)}, u32[]{:S(2)}) async-start(f32[8,256,128]{1,2,0:T(8,128)} %broadcast_in_dim.24), calls=%async_computation.3 | async-start | bytes 2097152 | tf_op jit(solution)/shard_map/all_to_all | solution.py:17
  107.2 0.1 copy.11
  107.3 15.4 %all-to-all-done.3 = f32[8,256,128]{1,2,0:T(8,128)S(1)} async-done(((f32[8,256,128]{1,2,0:T(8,128)}), f32[8,256,128]{1,2,0:T(8,128)S(1)}, u32[]{:S(2)}, u32[]{:S(2)}) %all-to-all-start.3) | async-done | bytes 1048608 | tf_op jit(solution)/shard_map/all_to_all | solution.py:17
  122.7 1.1 broadcast_in_dim.23
  123.8 3.6 %all-to-all-start.2 = ((f32[8,256,128]{1,2,0:T(8,128)}), f32[8,256,128]{1,2,0:T(8,128)S(1)}, u32[]{:S(2)}, u32[]{:S(2)}) async-start(f32[8,256,128]{1,2,0:T(8,128)} %broadcast_in_dim.23), calls=%async_computation.2 | async-start | bytes 2097152 | tf_op jit(solution)/shard_map/all_to_all | solution.py:17
  127.3 0.0 all-gather.7.cloned.1.call-start
  127.4 1.8 fusion.4
  129.2 16.9 %all-to-all-done.2 = f32[8,256,128]{1,2,0:T(8,128)S(1)} async-done(((f32[8,256,128]{1,2,0:T(8,128)}), f32[8,256,128]{1,2,0:T(8,128)S(1)}, u32[]{:S(2)}, u32[]{:S(2)}) %all-to-all-start.2) | async-done | bytes 1048608 | tf_op jit(solution)/shard_map/all_to_all | solution.py:17
  146.1 20.6 %all_to_all.42 = f32[4,256,128]{2,1,0:T(8,128)S(1)} all-to-all(f32[4,256,128]{2,1,0:T(8,128)S(1)} %broadcast_in_dim.26), channel_id=1, replica_groups=mesh['box'=16,'row'=4,'col'=8] {'row'}, dimensions={0} | all-to-all | bytes 1048576 | tf_op jit(solution)/shard_map/all_to_all | solution.py:17
  166.8 1.8 convolution_add_fusion
  168.6 0.1 copy.13
  168.7 0.1 broadcast_in_dim.27
  168.8 31.7 %all_to_all.43 = f32[8,256,128]{1,2,0:T(8,128)S(1)} all-to-all(f32[8,256,128]{1,2,0:T(8,128)S(1)} %broadcast_in_dim.27), channel_id=1, replica_groups=mesh['box'=16,'row'=4,'col'=8] {'col'}, dimensions={0} | all-to-all | bytes 2097152 | tf_op jit(solution)/shard_map/all_to_all | solution.py:17
  200.5 0.0 all-gather.5.cloned.1.call-done
  200.5 0.0 copy-start
  200.5 5.7 %fusion.5 = f32[256,768]{1,0:T(8,128)} fusion(f32[256,1024]{0,1:T(8,128)S(1)} %bitcast.45, f32[1024,768]{1,0:T(8,128)} %all-gather.5.cloned.1.call-done), kind=kOutput, calls=%fused_computation.13 | convolution fusion | flops 2415919104 | bytes 4980736 | tf_op jit(solution)/shard_map/dot_general | solution.py:31
  206.2 0.0 all-gather.7.cloned.1.call-update
  206.2 0.0 copy-done
  206.2 0.4 copy.8
  206.6 1.2 select_bitcast_fusion.1
  207.8 9.9 %all-gather.9.cloned.1.call-done = f32[1,768,1024]{2,1,0:T(8,128)} async-done(((f32[1,768,128]{2,1,0:T(8,128)}), f32[1,768,1024]{2,1,0:T(8,128)}) %all-gather.9.cloned.1.call-update) | async-done | bytes 3145744 | tf_op jit(solution)/shard_map/all_gather | solution.py:76
  217.6 54.1 %all-gather.7.cloned.1.call-done = f32[1024,768]{1,0:T(8,128)} async-done(((f32[256,768]{1,0:T(8,128)}), f32[1024,768]{1,0:T(8,128)}) %all-gather.7.cloned.1.call-update) | async-done | bytes 3145744 | tf_op jit(solution)/shard_map/all_gather | solution.py:71
  271.7 17.5 %maximum_add_fusion = f32[768,768]{0,1:T(8,128)S(1)} fusion(f32[768,384]{0,1:T(8,128)} %get-tuple-element.6, f32[768,384]{0,1:T(8,128)S(1)} %get-tuple-element.5, f32[1024,768]{1,0:T(8,128)} %all-gather.7.cloned.1.call-done, f32[1,768,1024]{2,1,0:T(8,128)} %all-gather.9.cloned.1.call-done), kind=kOutput, calls=%fused_computation.2 | convolution fusion | flops 7248936960 | bytes 11010048 | tf_op jit(solution)/shard_map/dot_general | solution.py:31
  289.2 3.0 %copy.14 = f32[1,768,2,384]{3,2,1,0:T(2,128)} copy(f32[1,768,2,384]{1,3,2,0:T(8,128)S(1)} %bitcast.41) | data formatting | bytes 4718592 | tf_op jit(solution)/shard_map/reshape | solution.py:77
  (3 shorter events, 0.0 us)
Async XLA Ops:
  6.5 24.2 %copy-start.1 = (f32[1,256,384]{2,1,0:T(8,128)S(1)}, f32[1,256,384]{2,1,0:T(8,128)}, u32[]{:S(2)}) copy-start(f32[1,256,384]{2,1,0:T(8,128)} %param.6) | copy-start | bytes 1179652
  6.5 7.0 %collective-permute-start = (f32[256,128]{1,0:T(8,128)}, f32[256,128]{1,0:T(8,128)S(1)}, u32[]{:S(2)}, u32[]{:S(2)}) collective-permute-start(f32[256,128]{1,0:T(8,128)} %bitcast.53), channel_id=1, source_target_pairs={{0,32},{32,0},{64,96},{96,64},{128,160},{160,128},{192,224},{224,1... | collective-permute-start | bytes 393224 | tf_op jit(solution)/shard_map/ppermute | solution.py:27
  32.0 29.6 %all-to-all-start.7 = ((f32[4,256,384]{2,1,0:T(8,128)}), f32[4,256,384]{2,1,0:T(8,128)S(1)}, u32[]{:S(2)}, u32[]{:S(2)}) async-start(f32[4,256,384]{2,1,0:T(8,128)} %broadcast_in_dim.29), calls=%async_computation.7 | async-start | bytes 3145728 | tf_op jit(solution)/shard_map/all_to_all | solution.py:17
  41.1 159.4 %all-gather.5.cloned.1.call-start = ((), (), s32[]{:S(2)}) async-start(), calls=%async_computation.8 | async-start | bytes 3932160 | tf_op jit(solution)/shard_map/all_gather | solution.py:67
  41.1 12.6 %collective-permute-start.1 = (f32[256,384]{1,0:T(8,128)S(1)}, f32[256,384]{1,0:T(8,128)S(1)}, u32[]{:S(2)}, u32[]{:S(2)}) collective-permute-start(f32[256,384]{1,0:T(8,128)S(1)} %bitcast.52), channel_id=1, source_target_pairs={{0,32},{32,0},{64,96},{96,64},{128,160},{160,128},{192,224},{224,1... | collective-permute-start | bytes 1179656 | tf_op jit(solution)/shard_map/ppermute | solution.py:27
  61.7 3.6 %copy-start.2 = (f32[1,256,128]{2,1,0:T(8,128)S(1)}, f32[1,256,128]{2,1,0:T(8,128)}, u32[]{:S(2)}) copy-start(f32[1,256,128]{2,1,0:T(8,128)} %param.7) | copy-start | bytes 393220
  64.5 153.1 %all-gather.9.cloned.1.call-start = ((), (), s32[]{:S(2)}) async-start(), calls=%async_computation.10 | async-start | bytes 3538944 | tf_op jit(solution)/shard_map/all_gather | solution.py:76
  66.1 13.8 %all-to-all-start.1 = ((f32[4,256,128]{2,1,0:T(8,128)}), f32[4,256,128]{2,1,0:T(8,128)S(1)}, u32[]{:S(2)}, u32[]{:S(2)}) async-start(f32[4,256,128]{2,1,0:T(8,128)} %broadcast_in_dim.22), calls=%async_computation.1 | async-start | bytes 1048576 | tf_op jit(solution)/shard_map/all_to_all | solution.py:17
  82.5 20.1 %all-to-all-start.4 = ((f32[4,256,128]{2,1,0:T(8,128)}), f32[4,256,128]{2,1,0:T(8,128)S(1)}, u32[]{:S(2)}, u32[]{:S(2)}) async-start(f32[4,256,128]{2,1,0:T(8,128)} %broadcast_in_dim.25), calls=%async_computation.4 | async-start | bytes 1048576 | tf_op jit(solution)/shard_map/all_to_all | solution.py:17
  103.6 19.1 %all-to-all-start.3 = ((f32[8,256,128]{1,2,0:T(8,128)}), f32[8,256,128]{1,2,0:T(8,128)S(1)}, u32[]{:S(2)}, u32[]{:S(2)}) async-start(f32[8,256,128]{1,2,0:T(8,128)} %broadcast_in_dim.24), calls=%async_computation.3 | async-start | bytes 2097152 | tf_op jit(solution)/shard_map/all_to_all | solution.py:17
  123.8 22.3 %all-to-all-start.2 = ((f32[8,256,128]{1,2,0:T(8,128)}), f32[8,256,128]{1,2,0:T(8,128)S(1)}, u32[]{:S(2)}, u32[]{:S(2)}) async-start(f32[8,256,128]{1,2,0:T(8,128)} %broadcast_in_dim.23), calls=%async_computation.2 | async-start | bytes 2097152 | tf_op jit(solution)/shard_map/all_to_all | solution.py:17
  127.3 144.4 %all-gather.7.cloned.1.call-start = ((), (), s32[]{:S(2)}) async-start(), calls=%async_computation.9 | async-start | bytes 3932160 | tf_op jit(solution)/shard_map/all_gather | solution.py:71
  200.5 5.7 %copy-start = (f32[1,768,384]{2,1,0:T(8,128)S(1)}, f32[1,768,384]{2,1,0:T(8,128)}, u32[]{:S(2)}) copy-start(f32[1,768,384]{2,1,0:T(8,128)} %param.4) | copy-start | bytes 3538948
Sparse Core Ops, SparseCore 0:
  64.6 52.6 all-gather.4
  119.4 98.2 all-gather.8
  219.7 51.9 all-gather.6
where the time goes:
time: 299 us
  waiting for transfers between devices  142 us (47%)
  blocking collectives  69.3 us (23%)
  starting transfers between devices  32.8 us (11%)
  matrix products  30.4 us (10%)
  between operations  13.3 us (4%)
  local copies, waits for them, and re-layouts  9.02 us (3%)
    all_to_all x3, blocking collectives, sent_to_all(): lax.all_to_all(jnp.broadcast_to(shard[None], (devices, *shard.shape)), ax...  69.3 us
    all_to_all x5, waiting for transfers between devices, sent_to_all(): lax.all_to_all(jnp.broadcast_to(shard[None], (devices, *shard.shape)), ax...  65.3 us
    all_gather x1, waiting for transfers between devices, local(): right_panel = lax.all_gather(carried, 'row', axis=0, tiled=True)  54.1 us
    dot_general x6, matrix products, panel_dot(): jnp.dot(piece, panel, precision=HIGH, preferred_element_type=jnp.float32)  30.4 us
    all_to_all x5, starting transfers between devices, sent_to_all(): lax.all_to_all(jnp.broadcast_to(shard[None], (devices, *shard.shape)), ax...  25 us
    ppermute x2, waiting for transfers between devices, swapped(): lax.ppermute(shard, axis, [(i, i ^ 1 << distance) for i in range(lax.axis...  11.9 us
    all_gather x1, waiting for transfers between devices, local(): lax.all_gather(own_ed, 'col', axis=1, tiled=True)  9.86 us
    ppermute x2, starting transfers between devices, swapped(): lax.ppermute(shard, axis, [(i, i ^ 1 << distance) for i in range(lax.axis...  7.65 us
  transfers between devices with their start and end apart: 10, of which 9 were waited for; matrix products, arithmetic and copies ran while one was open for 6% of the time, Pallas kernels for 0%

commit v1 on v0

v1 whole, which is shorter than its diff:
```python
import jax
import jax.numpy as jnp
from jax import lax
from jax.experimental import pallas as pl
from jax.experimental.pallas import tpu as pltpu
from jax.sharding import PartitionSpec as P

MESH = pl.DeviceIdType.MESH
F32 = jnp.float32
BF16 = jnp.bfloat16
SIDE = 4
MAX_COPIES = 160


def merge_kernel(ni, rows, cols, width, out_rows, dd_ref, de_ref, ed_ref, out_ref,
                 own_dd, partner_dd, de_parts, de_relay, de_other, ed, carr,
                 dd_hi, dd_lo, pd_hi, pd_lo, ed_hi, ed_lo, source, cat_a, cat_b,
                 send_sem, recv_sem, local_sem):
    box = lax.axis_index("box")
    row = lax.axis_index("row")
    col = lax.axis_index("col")
    core = row % 2
    x = col // 2
    y = row // 2 * 2 + col % 2
    other_box = box + 1 - 2 * (box % 2)
    yh = row // 2

    def near(dx=0, dy=0):
        there_x = (x + dx + SIDE) % SIDE
        there_y = (y + dy + SIDE) % SIDE
        return (box, there_y // 2 * 2 + core, there_x * 2 + there_y % 2)

    sibling = (box, yh * 2 + 1 - core, col)
    across = (other_box, row, col)
    y_pair = (box, row, x * 2 + 1 - col % 2)
    peers = [near(1), near(-1), near(0, 1), near(0, -1), across, sibling]

    made = [0]
    sent = []

    def send(src, dst, device):
        n = made[0]
        made[0] += 1
        copy = pltpu.make_async_remote_copy(
            src_ref=src, dst_ref=dst, send_sem=send_sem.at[n], recv_sem=recv_sem.at[n],
            device_id=device, device_id_type=MESH)
        copy.start()
        sent.append(copy)
        return n

    def arrived(n, ref, device):
        pltpu.make_async_remote_copy(
            src_ref=ref, dst_ref=ref, send_sem=send_sem.at[n], recv_sem=recv_sem.at[n],
            device_id=device, device_id_type=MESH).wait_recv()

    def block(buf, dx=0, dy=0, half=None, who=None):
        there_x = (x + dx + SIDE) % SIDE
        there_y = (y + dy + SIDE) % SIDE
        held_by = core if who is None else who
        start = (there_y // 2 * 2 + held_by) * rows
        size = rows
        if half is not None:
            size = rows // 2
            start = start + half * size
        return buf.at[there_x * 2 + there_y % 2, pl.ds(pl.multiple_of(start, 8), size), :]

    class Ring:
        def __init__(self, part, step):
            self.part = part
            self.step = step

        def first(self):
            own = self.part(0, None)
            self.up = send(own, own, self.step(1))
            self.down = send(own, own, self.step(-1))

        def second(self):
            arrived(self.up, self.part(-1, None), self.step(-1))
            low = self.part(-1, 0)
            self.up2 = send(low, low, self.step(1))
            arrived(self.down, self.part(1, None), self.step(1))
            high = self.part(1, 1)
            self.down2 = send(high, high, self.step(-1))

        def third(self):
            arrived(self.up2, self.part(2, 0), self.step(-1))
            arrived(self.down2, self.part(2, 1), self.step(1))

    def ring_x(buf, dy):
        return Ring(lambda d, half: block(buf, d, dy, half), lambda d: near(d))

    def ring_y(buf, dx):
        return Ring(lambda d, half: block(buf, dx, d, half), lambda d: near(0, d))

    shared = []

    def share(buf, dx, dy):
        mine = block(buf, dx, dy)
        shared.append((send(mine, mine, sibling), block(buf, dx, dy, None, 1 - core)))

    barrier = pltpu.get_barrier_semaphore()
    for peer in peers:
        pl.semaphore_signal(barrier, inc=1, device_id=peer, device_id_type=MESH)
    load_dd = pltpu.make_async_copy(dd_ref, block(own_dd), local_sem.at[0])
    load_de = pltpu.make_async_copy(de_ref, de_parts.at[0, yh], local_sem.at[1])
    load_ed = pltpu.make_async_copy(ed_ref, ed.at[col], local_sem.at[2])
    load_dd.start()
    load_de.start()
    load_ed.start()
    load_dd.wait()
    pl.semaphore_wait(barrier, len(peers))

    half_rows = rows // 2
    top = pl.ds(0, half_rows)
    bottom = pl.ds(half_rows, half_rows)

    z_dd = send(block(own_dd), block(partner_dd), across)
    px = ring_x(own_dd, 0)
    px.first()
    load_de.wait()
    de_up = send(de_parts.at[0, yh, top], de_relay.at[0], near(0, 1))
    de_down = send(de_parts.at[0, yh, bottom], de_relay.at[1], near(0, -1))
    z_de = send(de_parts.at[0, yh], de_parts.at[1, yh], across)
    py = {0: ring_y(own_dd, 0)}
    py[0].first()
    share(own_dd, 0, 0)
    load_ed.wait()

    arrived(z_dd, block(partner_dd), across)
    qy = ring_y(partner_dd, 0)
    qy.first()
    qx = {0: ring_x(partner_dd, 0)}
    qx[0].first()
    share(partner_dd, 0, 0)

    px.second()
    for d in (-1, 1):
        py[d] = ring_y(own_dd, d)
        py[d].first()
        share(own_dd, d, 0)
    from_below = (y - 1 + SIDE) % SIDE // 2
    from_above = (y + 1) % SIDE // 2
    arrived(de_up, de_relay.at[0], near(0, -1))
    de_up2 = send(de_relay.at[0], de_parts.at[0, from_below, top], near(0, 1))
    arrived(de_down, de_relay.at[1], near(0, 1))
    de_down2 = send(de_relay.at[1], de_parts.at[0, from_above, bottom], near(0, -1))

    qy.second()
    for d in (-1, 1):
        qx[d] = ring_x(partner_dd, d)
        qx[d].first()
        share(partner_dd, 0, d)

    ed_half = out_rows // 2
    ed_quarter = out_rows // 4

    def ed_part(flip, base):
        def part(d, half):
            there = (x + d + SIDE) % SIDE * 2 + (1 - col % 2 if flip else col % 2)
            if half is None:
                return ed.at[there, pl.ds(base, ed_half), :]
            return ed.at[there, pl.ds(base + half * ed_quarter, ed_quarter), :]
        return Ring(part, lambda d: near(d))

    ex = ed_part(False, ed_half)
    ex.first()

    py[0].second()
    qx[0].second()
    share(own_dd, 0, -1)
    share(own_dd, 0, 1)
    share(partner_dd, -1, 0)
    share(partner_dd, 1, 0)

    px.third()
    py[2] = ring_y(own_dd, 2)
    py[2].first()
    share(own_dd, 2, 0)
    qy.third()
    qx[2] = ring_x(partner_dd, 2)
    qx[2].first()
    share(partner_dd, 0, 2)

    arrived(de_up2, de_parts.at[0, 1 - yh, top], near(0, -1))
    arrived(de_down2, de_parts.at[0, 1 - yh, bottom], near(0, 1))
    z_de2 = send(de_parts.at[0, 1 - yh], de_parts.at[1, 1 - yh], across)

    for d in (-1, 1):
        py[d].second()
        qx[d].second()
        share(own_dd, d, -1)
        share(own_dd, d, 1)
        share(partner_dd, -1, d)
        share(partner_dd, 1, d)
    own_ed_up = ed.at[col, pl.ds(0, ed_half), :]
    e_pair = send(own_ed_up, own_ed_up, y_pair)
    ex.second()
    eo = ed_part(False, 0)
    eo.first()

    py[0].third()
    share(own_dd, 0, 2)
    qx[0].third()
    share(partner_dd, 2, 0)

    py[2].second()
    qx[2].second()
    share(own_dd, 2, -1)
    share(own_dd, 2, 1)
    share(partner_dd, -1, 2)
    share(partner_dd, 1, 2)
    for d in (-1, 1):
        py[d].third()
        qx[d].third()
        share(own_dd, d, 2)
        share(partner_dd, 2, d)
    arrived(z_de, de_parts.at[1, yh], across)
    arrived(z_de2, de_parts.at[1, 1 - yh], across)
    de_share = [send(de_parts.at[1 - core, h], de_other.at[h], sibling) for h in range(2)]

    py[2].third()
    qx[2].third()
    share(own_dd, 2, 2)
    share(partner_dd, 2, 2)
    for n, ref in shared:
        arrived(n, ref, sibling)
    for h in range(2):
        arrived(de_share[h], de_other.at[h], sibling)

    def split(value):
        high = value.astype(BF16)
        return high, (value - high.astype(F32)).astype(BF16)

    tile = 256
    blocks = ni // cols

    def split_all(buf, hi, lo, count):
        step = 128

        def body(i, carry):
            at = pl.ds(pl.multiple_of(i * step, step), step)
            for c in range(blocks):
                h, l = split(buf[c, at, :])
                hi[at, c * cols:(c + 1) * cols] = h
                lo[at, c * cols:(c + 1) * cols] = l
            return carry

        lax.fori_loop(0, count // step, body, 0)

    def put(cat, at, value):
        h, l = split(value)
        cat[at, :width] = h
        cat[at, width:] = l

    split_all(own_dd, dd_hi, dd_lo, ni)
    split_all(partner_dd, pd_hi, pd_lo, ni)

    for h in range(2):
        for who in range(2):
            at = pl.ds((h * 2 + who) * rows, rows)
            value = jnp.where(core == who, de_parts[core, h], de_other[h])
            source[at, :] = value
            put(cat_a, at, value)

    def product(hi, lo, cat, done, count=ni):
        def body(i, carry):
            at = pl.ds(pl.multiple_of(i * tile, tile), tile)
            both = jnp.dot(hi[at, :], cat[...], preferred_element_type=F32)
            cross = jnp.dot(lo[at, :], cat[:, :width], preferred_element_type=F32)
            done(at, both[:, :width] + (both[:, width:] + cross))
            return carry

        lax.fori_loop(0, count // tile, body, 0)

    def to_source(at, value):
        source[at, :] = value
        put(cat_b, at, value)

    def to_source_sum(at, value):
        value = source[at, :] + value
        source[at, :] = value
        put(cat_b, at, value)

    def to_a(at, value):
        put(cat_a, at, value)

    def to_b(at, value):
        put(cat_b, at, value)

    def to_carried(at, value):
        carr[core, at, :] = source[at, :] + value

    @pl.when(core == 0)
    def _():
        product(pd_hi, pd_lo, cat_a, to_source)

    @pl.when(core == 1)
    def _():
        cat_b[...] = cat_a[...]

    product(dd_hi, dd_lo, cat_b, to_a)
    ex.third()
    arrived(e_pair, ed.at[x * 2 + 1 - col % 2, pl.ds(0, ed_half), :], y_pair)
    ep = ed_part(True, 0)
    ep.first()
    eo.second()

    def low_rows(d, flip):
        there = (x + d + SIDE) % SIDE * 2 + (1 - col % 2 if flip else col % 2)
        return ed.at[there, pl.ds(ed_half, ed_half), :]

    e_last = [(send(low_rows(d, False), low_rows(d, False), y_pair), low_rows(d, True))
              for d in (0, 1, -1, 2)]
    product(pd_hi, pd_lo, cat_a, to_b)
    eo.third()
    ep.second()
    product(dd_hi, dd_lo, cat_b, to_a)
    product(pd_hi, pd_lo, cat_a, to_source_sum)
    product(dd_hi, dd_lo, cat_b, to_a)
    ep.third()
    for n, ref in e_last:
        arrived(n, ref, y_pair)
    product(pd_hi, pd_lo, cat_a, to_carried)
    mine = send(carr.at[core], carr.at[core], sibling)

    split_all(ed, ed_hi, ed_lo, out_rows)

    def fill(kind):
        def body(i, carry):
            at = pl.ds(pl.multiple_of(i * 128, 128), 128)
            put(cat_b, at, carr[kind, at, :])
            return carry

        lax.fori_loop(0, ni // 128, body, 0)

    def final(kind):
        slot = (kind + box) % 2

        def done(at, value):
            out_ref[slot, at, :] = value

        fill(kind)
        product(ed_hi, ed_lo, cat_b, done, out_rows)

    final(core)
    arrived(mine, carr.at[1 - core], sibling)
    final(1 - core)

    for copy in sent:
        copy.wait_send()


def local(ext_ext, ext_int, int_ext, int_int):
    dd, de, ed, ee = int_int[0], int_ext[0], ext_int[0], ext_ext[0]
    rows, cols = dd.shape
    width = de.shape[1]
    out_rows = ed.shape[0]
    ni = rows * lax.axis_size("row")
    blocks = ni // cols

    def body(*refs):
        merge_kernel(ni, rows, cols, width, out_rows, *refs)

    product = pl.pallas_call(
        body,
        out_shape=jax.ShapeDtypeStruct((2, out_rows, width), F32),
        in_specs=[pl.BlockSpec(memory_space=pl.ANY)] * 3,
        out_specs=pl.BlockSpec(memory_space=pltpu.VMEM),
        scratch_shapes=[
            pltpu.VMEM((blocks, ni, cols), F32),
            pltpu.VMEM((blocks, ni, cols), F32),
            pltpu.VMEM((2, 2, rows, width), F32),
            pltpu.VMEM((2, rows // 2, width), F32),
            pltpu.VMEM((2, rows, width), F32),
            pltpu.VMEM((blocks, out_rows, cols), F32),
            pltpu.VMEM((2, ni, width), F32),
            pltpu.VMEM((ni, ni), BF16),
            pltpu.VMEM((ni, ni), BF16),
            pltpu.VMEM((ni, ni), BF16),
            pltpu.VMEM((ni, ni), BF16),
            pltpu.VMEM((out_rows, ni), BF16),
            pltpu.VMEM((out_rows, ni), BF16),
            pltpu.VMEM((ni, width), F32),
            pltpu.VMEM((ni, 2 * width), BF16),
            pltpu.VMEM((ni, 2 * width), BF16),
            pltpu.SemaphoreType.DMA((MAX_COPIES,)),
            pltpu.SemaphoreType.DMA((MAX_COPIES,)),
            pltpu.SemaphoreType.DMA((3,)),
        ],
        compiler_params=pltpu.CompilerParams(
            collective_id=0, has_side_effects=True, vmem_limit_bytes=60 * 2**20),
    )(dd, de, ed)
    slot = lax.broadcasted_iota(jnp.int32, (1, 2, 1), 1)
    keep = slot == lax.axis_index("box") % 2
    merged = jnp.where(keep, ee[:, None, :], 0.0) + jnp.swapaxes(product, 0, 1)
    return merged[None]


def solution(mesh):
    placed = P("box", "row", "col")
    return jax.shard_map(
        local, mesh=mesh, in_specs=(placed,) * 4, out_specs=P("box", "row", None, "col"),
        check_vma=False)
```

time: 299 us -> 91.2 us (0.31)
  waiting for transfers between devices: 142 us -> 0 us
  Pallas kernels: 0 us -> 84.2 us
  blocking collectives: 69.3 us -> 0 us
  starting transfers between devices: 32.8 us -> 0 us
  matrix products: 30.4 us -> 0 us
  between operations: 13.3 us -> 0.02 us
  local copies, waits for them, and re-layouts: 9.02 us -> 3.23 us
    pallas_call x0 -> x1, Pallas kernels: none -> 84.2 us  [local(): pl.pallas_call(body, out_shape=jax.ShapeDtypeStruct((2, out_rows, width),...]
    all_to_all x3 -> x0, blocking collectives: 69.3 us -> none  [sent_to_all(): lax.all_to_all(jnp.broadcast_to(shard[None], (devices, *shard.shape)), ax...]
    all_to_all x5 -> x0, waiting for transfers between devices: 65.3 us -> none  [sent_to_all(): lax.all_to_all(jnp.broadcast_to(shard[None], (devices, *shard.shape)), ax...]
    all_gather x3 -> x0, waiting for transfers between devices: 64 us -> none  [the longest x1 54.1 us: local(): right_panel = lax.all_gather(carried, 'row', axis=0, tiled=True)]
    dot_general x6 -> x0, matrix products: 30.4 us -> none  [panel_dot(): jnp.dot(piece, panel, precision=HIGH, preferred_element_type=jnp.float32)]
    all_to_all x5 -> x0, starting transfers between devices: 25 us -> none  [sent_to_all(): lax.all_to_all(jnp.broadcast_to(shard[None], (devices, *shard.shape)), ax...]
    ppermute x2 -> x0, waiting for transfers between devices: 11.9 us -> none  [swapped(): lax.ppermute(shard, axis, [(i, i ^ 1 << distance) for i in range(lax.axis...]
    ppermute x2 -> x0, starting transfers between devices: 7.65 us -> none  [swapped(): lax.ppermute(shard, axis, [(i, i ^ 1 << distance) for i in range(lax.axis...]
  transfers between devices with their start and end apart: 10 -> 0, of which waited for: 9 -> 0; matrix products, arithmetic and copies ran while one was open for 6% -> 0% of each run, Pallas kernels for 0% -> 0%
where the time goes in v1:
time: 91.2 us; the launch traced here: 89.4 us
  Pallas kernels  84.2 us (92%)
  local copies, waits for them, and re-layouts  3.23 us (4%)
  other arithmetic  1.93 us (2%)
    pallas_call x1, Pallas kernels, local(): pl.pallas_call(body, out_shape=jax.ShapeDtypeStruct((2, out_rows, width),...  84.2 us
    broadcast_in_dim x1, local copies, waits for them, and re-layouts, local(): return merged[None]  3.23 us
    broadcast_in_dim x1, other arithmetic, local(): return merged[None]  1.92 us

profile of v1, /device:TPU:1, one launch (start us, length us, event | category | flops | bytes accessed | tf_op | source)
XLA Modules:
  0.0 89.4 jit_solution(13760470539737572412)
XLA Ops:
  0.0 0.0 copy-start
  0.0 84.2 %shard_map.46 = f32[2,768,384]{2,1,0:T(8,128)} custom-call(f32[256,128]{1,0:T(8,128)} %bitcast.13, f32[256,384]{1,0:T(8,128)} %bitcast.11, f32[768,128]{1,0:T(8,128)} %bitcast.12), custom_call_target="tpu_custom_call" | custom-call | tf_op jit(solution)/shard_map/pallas_call | solution.py:364
  84.2 0.0 copy-done
  84.3 1.9 %fusion = f32[1,768,2,384]{3,1,2,0:T(8,128)S(1)} fusion(f32[2,768,384]{2,1,0:T(8,128)} %shard_map.46, f32[768,384]{1,0:T(8,128)S(1)} %bitcast.10, pred[2]{0:T(512)(128)(4,1)S(1)} %iota_compare_fusion), kind=kLoop, calls=%fused_computation.1 | loop fusion | flops 1179648 | bytes 5898242 | tf_op jit(solution)/shard_map/broadcast_in_dim | solution.py:396
  86.2 3.2 %copy.5 = f32[1,768,2,384]{3,2,1,0:T(2,128)} copy(f32[1,768,2,384]{3,1,2,0:T(8,128)S(1)} %fusion) | data formatting | bytes 4718592 | tf_op jit(solution)/shard_map/broadcast_in_dim | solution.py:396
  (1 shorter events, 0.0 us)
Async XLA Ops:
  0.0 84.2 %copy-start = (f32[1,768,384]{2,1,0:T(8,128)S(1)}, f32[1,768,384]{2,1,0:T(8,128)}, u32[]{:S(2)}) copy-start(f32[1,768,384]{2,1,0:T(8,128)} %param.4) | copy-start | bytes 3538948

commit v2 on v1

v2 whole, which is shorter than its diff:
```python
import jax
import jax.numpy as jnp
from jax import lax
from jax.experimental import pallas as pl
from jax.experimental.pallas import tpu as pltpu
from jax.sharding import PartitionSpec as P

MESH = pl.DeviceIdType.MESH
F32 = jnp.float32
BF16 = jnp.bfloat16
SIDE = 4
MAX_COPIES = 224
RELAY_AT = (2, 2, 4, 5, 6, 12, 12)
ED_UP = 352


def merge_kernel(ni, rows, cols, width, out_rows, dd_ref, de_ref, ed_ref, ee_ref, out_ref,
                 own_dd, partner_dd, de_parts, de_other, ed, carr,
                 dd_hi, dd_lo, pd_hi, pd_lo, ed_hi, ed_lo, source, cat_a, cat_b, ee,
                 send_sem, recv_sem, local_sem):
    box = lax.axis_index("box")
    row = lax.axis_index("row")
    col = lax.axis_index("col")
    core = row % 2
    x = col // 2
    y = row // 2 * 2 + col % 2
    other_box = box + 1 - 2 * (box % 2)
    yh = row // 2

    def near(dx=0, dy=0):
        there_x = (x + dx + SIDE) % SIDE
        there_y = (y + dy + SIDE) % SIDE
        return (box, there_y // 2 * 2 + core, there_x * 2 + there_y % 2)

    sibling = (box, yh * 2 + 1 - core, col)
    across = (other_box, row, col)
    y_pair = (box, row, x * 2 + 1 - col % 2)
    far_x, far_y = near(2), near(0, 2)
    peers = [near(1), near(-1), near(0, 1), near(0, -1), far_x, far_y, across, sibling]

    made = [0]
    sent = []

    def send(src, dst, device):
        n = made[0]
        made[0] += 1
        copy = pltpu.make_async_remote_copy(
            src_ref=src, dst_ref=dst, send_sem=send_sem.at[n], recv_sem=recv_sem.at[n],
            device_id=device, device_id_type=MESH)
        copy.start()
        sent.append(copy)
        return n

    def arrived(n, ref, device):
        pltpu.make_async_remote_copy(
            src_ref=ref, dst_ref=ref, send_sem=send_sem.at[n], recv_sem=recv_sem.at[n],
            device_id=device, device_id_type=MESH).wait_recv()

    def block(buf, dx=0, dy=0, piece=(0, 1), who=None):
        there_x = (x + dx + SIDE) % SIDE
        there_y = (y + dy + SIDE) % SIDE
        held_by = core if who is None else who
        at, of = piece
        size = rows // of
        start = (there_y // 2 * 2 + held_by) * rows + at * size
        return buf.at[there_x * 2 + there_y % 2, pl.ds(pl.multiple_of(start, 8), size), :]

    class Ring:
        def __init__(self, part, step):
            self.part = part
            self.step = step

        def first(self):
            own = self.part(0, None)
            self.up = send(own, own, self.step(1))
            self.down = send(own, own, self.step(-1))

        def second(self):
            arrived(self.up, self.part(-1, None), self.step(-1))
            low = self.part(-1, 0)
            self.up2 = send(low, low, self.step(1))
            arrived(self.down, self.part(1, None), self.step(1))
            high = self.part(1, 1)
            self.down2 = send(high, high, self.step(-1))

        def third(self):
            arrived(self.up2, self.part(2, 0), self.step(-1))
            arrived(self.down2, self.part(2, 1), self.step(1))

    class Direct:
        def __init__(self, part, step):
            self.part = part
            self.step = step

        def first(self):
            own = self.part(0)
            self.sent = {d: send(own, own, self.step(d)) for d in (1, -1, 2)}

        def second(self):
            for d in (1, -1):
                arrived(self.sent[d], self.part(-d), self.step(-d))

        def third(self):
            arrived(self.sent[2], self.part(2), self.step(2))

    def direct_x(buf, piece=(0, 1)):
        return Direct(lambda d: block(buf, d, 0, piece), lambda d: near(d))

    def direct_y(buf, piece=(0, 1)):
        return Direct(lambda d: block(buf, 0, d, piece), lambda d: near(0, d))

    def ring_x(buf, dy, piece=(0, 1)):
        at, of = piece

        def part(d, half):
            if half is None:
                return block(buf, d, dy, piece)
            return block(buf, d, dy, (at * 2 + half, of * 2))

        return Ring(part, near)

    def ring_y(buf, dx, piece=(0, 1)):
        at, of = piece

        def part(d, half):
            if half is None:
                return block(buf, dx, d, piece)
            return block(buf, dx, d, (at * 2 + half, of * 2))

        return Ring(part, lambda d: near(0, d))

    shared = {}

    def share(buf, dx, dy):
        mine = block(buf, dx, dy)
        whose = shared.setdefault(id(buf), [])
        whose.append((send(mine, mine, sibling), block(buf, dx, dy, who=1 - core)))

    def shares_arrived(buf):
        for n, ref in shared[id(buf)]:
            arrived(n, ref, sibling)

    def split(value):
        high = value.astype(BF16)
        return high, (value - high.astype(F32)).astype(BF16)

    tile = 256
    blocks = ni // cols

    def split_all(buf, hi, lo, count):
        step = 128

        def body(i, carry):
            at = pl.ds(pl.multiple_of(i * step, step), step)
            for c in range(blocks):
                h, l = split(buf[c, at, :])
                hi[at, c * cols:(c + 1) * cols] = h
                lo[at, c * cols:(c + 1) * cols] = l
            return carry

        lax.fori_loop(0, count // step, body, 0)

    def put(cat, at, value):
        h, l = split(value)
        cat[at, :width] = h
        cat[at, width:] = l

    barrier = pltpu.get_barrier_semaphore()
    for peer in peers:
        pl.semaphore_signal(barrier, inc=1, device_id=peer, device_id_type=MESH)
    load_dd = pltpu.make_async_copy(dd_ref, block(own_dd), local_sem.at[0])
    load_de = pltpu.make_async_copy(de_ref, de_parts.at[0, yh], local_sem.at[1])
    load_ed = pltpu.make_async_copy(ed_ref, ed.at[col], local_sem.at[2])
    load_dd.start()
    load_de.start()
    load_ed.start()
    load_ee = pltpu.make_async_copy(ee_ref, ee, local_sem.at[3])
    load_ee.start()
    load_dd.wait()
    pl.semaphore_wait(barrier, len(peers))

    TOP, BOTTOM = (0, 2), (1, 2)

    def ed_ring(flip, base, size):
        def part(d, half):
            there = (x + d + SIDE) % SIDE * 2 + (1 - col % 2 if flip else col % 2)
            if half is None:
                return ed.at[there, pl.ds(base, size), :]
            return ed.at[there, pl.ds(base + half * (size // 2), size // 2), :]
        return Ring(part, near)

    ed_up = ED_UP
    ed_low = out_rows - ed_up
    z_dd = send(block(own_dd), block(partner_dd), across)
    px = direct_x(own_dd, TOP)
    px.first()
    oy = direct_y(own_dd, BOTTOM)
    oy.first()
    ox = {0: ring_x(own_dd, 0, BOTTOM)}
    ox[0].first()
    py = {0: ring_y(own_dd, 0, TOP)}
    py[0].first()
    load_de.wait()
    z_de = send(de_parts.at[0, yh], de_parts.at[1, yh], across)
    share(own_dd, 0, 0)
    load_ed.wait()
    load_ee.wait()

    def to_py(d):
        py[d] = ring_y(own_dd, d, TOP)
        py[d].first()

    def to_ox(d):
        ox[d] = ring_x(own_dd, d, BOTTOM)
        ox[d].first()

    arrived(z_dd, block(partner_dd), across)
    qy = direct_y(partner_dd)
    qy.first()
    own = block(partner_dd)
    qx_up = send(own, own, near(1))
    qx_down = send(own, own, near(-1))
    share(partner_dd, 0, 0)

    px.second()
    to_py(-1)
    to_py(1)
    oy.second()
    to_ox(-1)
    to_ox(1)
    px.third()
    to_py(2)
    oy.third()
    to_ox(2)
    y_de = send(de_parts.at[0, yh], de_parts.at[0, yh], far_y)

    ox[0].second()
    for d in (-1, 1):
        share(own_dd, d, 0)
    py[0].second()
    for d in (-1, 1):
        share(own_dd, 0, d)

    qx = {}

    def to_qx(d):
        qx[d] = ring_x(partner_dd, d)
        qx[d].first()
        share(partner_dd, 0, d)

    qy.second()
    to_qx(-1)
    to_qx(1)
    qy.third()
    to_qx(2)
    ox[0].third()
    z_row = send(block(own_dd, 2, 0), block(partner_dd, 2, 0), across)
    share(own_dd, 2, 0)
    arrived(qx_up, block(partner_dd, -1, 0), near(-1))
    share(partner_dd, -1, 0)
    arrived(qx_down, block(partner_dd, 1, 0), near(1))
    share(partner_dd, 1, 0)

    for d in (-1, 1):
        py[d].second()
        ox[d].second()
    py[0].third()
    share(own_dd, 0, 2)
    py[2].second()
    ox[2].second()
    arrived(y_de, de_parts.at[0, 1 - yh], far_y)
    z_de2 = send(de_parts.at[0, 1 - yh], de_parts.at[1, 1 - yh], across)


    for d in (-1, 1):
        qx[d].second()
        for e in (-1, 1):
            share(partner_dd, e, d)
    for d in (-1, 1):
        for e in (-1, 1):
            share(own_dd, d, e)
    qx[2].second()
    for e in (-1, 1):
        share(partner_dd, e, 2)
    own_ed_up = ed.at[col, pl.ds(0, ed_up), :]
    e_pair = send(own_ed_up, own_ed_up, y_pair)
    ex = ed_ring(False, ed_up, ed_low)
    ex.first()
    eo = ed_ring(False, 0, ed_up)
    eo.first()
    for d in (-1, 1):
        py[d].third()
        ox[d].third()
    for d in (-1, 1):
        share(own_dd, d, 2)
        share(own_dd, 2, d)
    py[2].third()
    ox[2].third()
    share(own_dd, 2, 2)
    shares_arrived(own_dd)
    split_all(own_dd, dd_hi, dd_lo, ni)
    for d in (-1, 1):
        qx[d].third()
        share(partner_dd, 2, d)
    arrived(z_row, block(partner_dd, 2, 0), across)
    share(partner_dd, 2, 0)
    arrived(z_de, de_parts.at[1, yh], across)
    arrived(z_de2, de_parts.at[1, 1 - yh], across)
    de_share = [send(de_parts.at[1 - core, h], de_other.at[h], sibling) for h in range(2)]
    qx[2].third()
    share(partner_dd, 2, 2)

    shares_arrived(partner_dd)
    split_all(partner_dd, pd_hi, pd_lo, ni)
    for h in range(2):
        arrived(de_share[h], de_other.at[h], sibling)

    for h in range(2):
        for who in range(2):
            at = pl.ds((h * 2 + who) * rows, rows)
            value = jnp.where(core == who, de_parts[core, h], de_other[h])
            source[at, :] = value
            put(cat_a, at, value)

    def product(hi, lo, cat, done, count=ni, first=0):
        def body(i, carry):
            at = pl.ds(pl.multiple_of(i * tile, tile), tile)
            both = jnp.dot(hi[at, :], cat[...], preferred_element_type=F32)
            cross = jnp.dot(lo[at, :], cat[:, :width], preferred_element_type=F32)
            done(at, both[:, :width] + (both[:, width:] + cross))
            return carry

        lax.fori_loop(first // tile, count // tile, body, 0)

    def to_source(at, value):
        source[at, :] = value
        put(cat_b, at, value)

    def to_source_sum(at, value):
        value = source[at, :] + value
        source[at, :] = value
        put(cat_b, at, value)

    def to_a(at, value):
        put(cat_a, at, value)

    def to_b(at, value):
        put(cat_b, at, value)

    def to_carried(at, value):
        value = source[at, :] + value
        carr[core, at, :] = value
        put(cat_b, at, value)

    @pl.when(core == 0)
    def _():
        product(pd_hi, pd_lo, cat_a, to_source)

    @pl.when(core == 1)
    def _():
        cat_b[...] = cat_a[...]

    e_last = []

    def low_rows(d, flip):
        there = (x + d + SIDE) % SIDE * 2 + (1 - col % 2 if flip else col % 2)
        return ed.at[there, pl.ds(ed_up, ed_low), :]

    def low_to_pair(d):
        e_last.append((send(low_rows(d, False), low_rows(d, False), y_pair), low_rows(d, True)))

    rings = {}

    def upper_of_pair():
        arrived(e_pair, ed.at[x * 2 + 1 - col % 2, pl.ds(0, ed_up), :], y_pair)
        rings["ep"] = ed_ring(True, 0, ed_up)
        rings["ep"].first()
        low_to_pair(0)

    def lower_second():
        ex.second()
        low_to_pair(1)
        low_to_pair(-1)

    def lower_third():
        ex.third()
        low_to_pair(2)

    steps = [upper_of_pair, lower_second, lambda: eo.second(), lower_third,
             lambda: rings["ep"].second(), lambda: eo.third(), lambda: rings["ep"].third()]
    chain = [(dd_hi, dd_lo, cat_b, to_a), (pd_hi, pd_lo, cat_a, to_b),
             (dd_hi, dd_lo, cat_b, to_a), (pd_hi, pd_lo, cat_a, to_source_sum),
             (dd_hi, dd_lo, cat_b, to_a), (pd_hi, pd_lo, cat_a, to_carried)]
    half = ni // 2

    def half_of(kind, n):
        return carr.at[kind, pl.ds(n * half, half), :]

    def send_half(n):
        return send(half_of(core, n), half_of(core, n), sibling)

    for n in range(2 * len(chain)):
        for step, when in zip(steps, RELAY_AT):
            if when == n:
                step()
        if n == 2 * len(chain) - 1:
            mine = [send_half(0)]
        product(*chain[n // 2], half * (n % 2 + 1), half * (n % 2))
    mine.append(send_half(1))
    for step, when in zip(steps, RELAY_AT):
        if when == 2 * len(chain):
            step()
    for n, ref in e_last:
        arrived(n, ref, y_pair)

    split_all(ed, ed_hi, ed_lo, out_rows)

    def fill(kind):
        def body(i, carry):
            at = pl.ds(pl.multiple_of(i * 128, 128), 128)
            put(cat_b, at, carr[kind, at, :])
            return carry

        lax.fori_loop(0, ni // 128, body, 0)

    def final(kind):
        slot = (kind + box) % 2

        def done(at, value):
            value = jnp.where(kind == 0, ee[at, :], 0.0) + value
            out_ref[slot, at, :] = value

        product(ed_hi, ed_lo, cat_b, done, out_rows)

    final(core)
    for n in range(2):
        arrived(mine[n], half_of(1 - core, n), sibling)
    fill(1 - core)
    final(1 - core)

    for copy in sent:
        copy.wait_send()


def local(ext_ext, ext_int, int_ext, int_int):
    dd, de, ed, ee = int_int[0], int_ext[0], ext_int[0], ext_ext[0]
    rows, cols = dd.shape
    width = de.shape[1]
    out_rows = ed.shape[0]
    ni = rows * lax.axis_size("row")
    blocks = ni // cols

    def body(*refs):
        merge_kernel(ni, rows, cols, width, out_rows, *refs)

    product = pl.pallas_call(
        body,
        out_shape=jax.ShapeDtypeStruct((2, out_rows, width), F32),
        in_specs=[pl.BlockSpec(memory_space=pl.ANY)] * 4,
        out_specs=pl.BlockSpec(memory_space=pltpu.VMEM),
        scratch_shapes=[
            pltpu.VMEM((blocks, ni, cols), F32),
            pltpu.VMEM((blocks, ni, cols), F32),
            pltpu.VMEM((2, 2, rows, width), F32),
            pltpu.VMEM((2, rows, width), F32),
            pltpu.VMEM((blocks, out_rows, cols), F32),
            pltpu.VMEM((2, ni, width), F32),
            pltpu.VMEM((ni, ni), BF16),
            pltpu.VMEM((ni, ni), BF16),
            pltpu.VMEM((ni, ni), BF16),
            pltpu.VMEM((ni, ni), BF16),
            pltpu.VMEM((out_rows, ni), BF16),
            pltpu.VMEM((out_rows, ni), BF16),
            pltpu.VMEM((ni, width), F32),
            pltpu.VMEM((ni, 2 * width), BF16),
            pltpu.VMEM((ni, 2 * width), BF16),
            pltpu.VMEM((out_rows, width), F32),
            pltpu.SemaphoreType.DMA((MAX_COPIES,)),
            pltpu.SemaphoreType.DMA((MAX_COPIES,)),
            pltpu.SemaphoreType.DMA((4,)),
        ],
        compiler_params=pltpu.CompilerParams(
            collective_id=0, has_side_effects=True, vmem_limit_bytes=60 * 2**20),
    )(dd, de, ed, ee)
    return jnp.swapaxes(product, 0, 1)[None]


def solution(mesh):
    placed = P("box", "row", "col")
    return jax.shard_map(
        local, mesh=mesh, in_specs=(placed,) * 4, out_specs=P("box", "row", None, "col"),
        check_vma=False)
```

time: 91.2 us -> 86.2 us (0.945); the launches traced: 89.4 us -> 85.4 us
  Pallas kernels: 84.2 us -> 80.5 us
  other arithmetic: 1.93 us -> 0 us
  local copies, waits for them, and re-layouts: 3.23 us -> 4.89 us
    pallas_call x1, Pallas kernels: 84.2 us -> 80.5 us  [local(): pl.pallas_call(body, out_shape=jax.ShapeDtypeStruct((2, out_rows, width),...]
    broadcast_in_dim x1 -> x0, other arithmetic: 1.92 us -> none  [local(): return merged[None]]
    broadcast_in_dim x1, local copies, waits for them, and re-layouts: 3.23 us -> 4.89 us  [local(): return jnp.swapaxes(product, 0, 1)[None]]
where the time goes in v2:
time: 86.2 us; the launch traced here: 85.4 us
  Pallas kernels  80.5 us (93%)
  local copies, waits for them, and re-layouts  4.89 us (6%)
    pallas_call x1, Pallas kernels, local(): pl.pallas_call(body, out_shape=jax.ShapeDtypeStruct((2, out_rows, width),...  80.5 us
    broadcast_in_dim x1, local copies, waits for them, and re-layouts, local(): return jnp.swapaxes(product, 0, 1)[None]  4.89 us

profile of v2, /device:TPU:1, one launch (start us, length us, event | category | flops | bytes accessed | tf_op | source)
XLA Modules:
  0.0 85.4 jit_solution(6063144207774725908)
XLA Ops:
  0.0 80.5 %shard_map.46 = f32[2,768,384]{2,1,0:T(8,128)} custom-call(f32[256,128]{1,0:T(8,128)} %bitcast.11, f32[256,384]{1,0:T(8,128)} %bitcast.9, f32[768,128]{1,0:T(8,128)} %bitcast.10, f32[768,384]{1,0:T(8,128)} %bitcast.8), custom_call_target="tpu_custom_call" | custom-call | tf_op jit(solution)/shard_map/pallas_call | solution.py:456
  80.5 4.9 %copy.5 = f32[1,768,2,384]{3,2,1,0:T(2,128)} copy(f32[1,768,2,384]{3,1,2,0:T(8,128)} %bitcast.7) | data formatting | bytes 4718592 | tf_op jit(solution)/shard_map/broadcast_in_dim | solution.py:485
